TPU v7x, 32 devices: a whole 2x2x4 slice. The times are simulated.
32 devices in a mesh: fluid: 8 (over z, y), grp: 4 (over x, core).
Axes of the slice: x: 2, y: 2, z: 4, core: 2. Of those that a mesh axis runs over, the one named last changes fastest.
Arguments:
- acoustic_modes: bfloat16 [262144, 400], P(('fluid', 'grp')), may hold values from -6 to 6
- shell_modes: bfloat16 [8192, 300], P('fluid'), may hold values from -0.0012207031 to 0.0012207031
- wet_counts: int32 [32], P(('fluid', 'grp')), may hold values from 1 to 2048, 26214 in all
- fluid_nodes: int32 [65536], P(('fluid', 'grp')), may hold values from 0 to 8191
- shell_nodes: int32 [65536], P(('fluid', 'grp')), may hold values from 0 to 1023
- wet_area: float32 [65536], P(('fluid', 'grp')), may hold values from 0.15 to 0.6
- shell_freq: float32 [300], replicated, may hold values from 1 to 2
- shell_loss: float32 [300], replicated, may hold values from 0.2 to 0.5
- cavity_freq: float32 [400], replicated, may hold values from 1 to 2
- cavity_loss: float32 [400], replicated, may hold values from 0.2 to 0.5
- freqs: float32 [64], replicated, may hold values from 0.7 to 2.2
- modal_force: float32 [300], replicated, may hold values from -1.5 to 1.5
- cavity_source: float32 [400], replicated, may hold values from -1.5 to 1.5
Outputs:
- pressure: bfloat16 [262144, 128], P(('fluid', 'grp'))
- modal_structure: float32 [2, 64, 300], P(None, 'grp')
Inputs may be any that keep to these rules, and one draw needn't show every extreme that they name: `wet_counts`: slots 0 to count - 1 of a device's 2048 interface slots are live, the others are ignored. `fluid_nodes`: numbered within the device's own 8192 cavity rows. `shell_nodes`: numbered within the 1024 shell rows of the device's fluid index.
All inputs are finite; a program needn't handle non-finite values.
Results may differ from a plain program's by a relative error of at most 0.0055.
Values may be sent and summed in bfloat16 or wider, within the bound.
No kernel may reach another device: no remote copies, remote signals or barrier semaphores. Data moves between devices by JAX's collectives and lax.ppermute only.
A program may use at most 64 MiB of HBM per device.

v0:
```python
import math

import jax
import jax.numpy as jnp
from jax import lax
from jax.sharding import PartitionSpec as P

SECTIONS = 4


HIGH = lax.Precision.HIGHEST


def divide_complex(real_part, imag_part, denom_real, denom_imag):
    scale = denom_real * denom_real + denom_imag * denom_imag
    return (
        (real_part * denom_real + imag_part * denom_imag) / scale,
        (imag_part * denom_real - real_part * denom_imag) / scale,
    )


def modal_terms(omega, loss, freqs):
    stiff = omega * omega
    real_part = stiff[None, :] - (freqs * freqs)[:, None]
    imag_part = jnp.broadcast_to((loss * stiff)[None, :], real_part.shape)
    return (real_part, imag_part)


def couple_rows(shell_modes, wet_rows, node_rows, live_counts):
    depth, width, cavity = wet_rows.shape
    block = math.gcd(depth, 256)
    result = jnp.zeros((shell_modes.shape[1], cavity), jnp.float32)
    source = 0

    def add_block(number, carry, source=source):
        first = number * block
        piece = lax.dynamic_slice(wet_rows, (first, source, 0), (block, 1, cavity)).reshape(
            block, cavity
        )
        picks = lax.dynamic_slice(node_rows, (first, source), (block, 1)).reshape(block)
        shell_rows = shell_modes[picks]
        return carry + lax.dot_general(
            shell_rows, piece, (((0,), (0,)), ((), ())), preferred_element_type=jnp.float32
        )

    result = lax.fori_loop(0, (live_counts[source] + block - 1) // block, add_block, result)
    return result


def on_device(
    acoustic_modes,
    shell_modes,
    wet_counts,
    fluid_nodes,
    shell_nodes,
    wet_area,
    shell_freq,
    shell_loss,
    cavity_freq,
    cavity_loss,
    freqs,
    modal_force,
    cavity_source,
):
    groups = lax.axis_size("grp")
    member = lax.axis_index("grp")
    slots = fluid_nodes.shape[0]
    freq_total = freqs.shape[0]
    freq_count = freq_total // groups
    count = wet_counts[0]
    live = (jnp.arange(slots, dtype=jnp.int32) < count).astype(jnp.float32)
    wet_rows = (
        wet_area[:, None] * acoustic_modes[fluid_nodes].astype(jnp.float32) * live[:, None]
    ).astype(jnp.bfloat16)
    partial_sum = couple_rows(shell_modes, wet_rows[:, None, :], shell_nodes[:, None], [count])
    ds_re, ds_im = modal_terms(shell_freq, shell_loss, freqs)
    da_re, da_im = modal_terms(cavity_freq, cavity_loss, freqs)
    free_re, free_im = divide_complex(
        jnp.broadcast_to(cavity_source[None, :], da_re.shape), jnp.zeros_like(da_re), da_re, da_im
    )
    free_amps = jnp.concatenate([free_re, free_im], 0).astype(jnp.bfloat16)
    free_field = lax.dot_general(
        acoustic_modes, free_amps, (((1,), (1,)), ((), ())), preferred_element_type=jnp.float32
    )
    squared = (freqs * freqs)[:, None]
    coupling = lax.psum(partial_sum, ("fluid", "grp"))
    start = member * freq_count

    def own_rows(values):
        return lax.dynamic_slice_in_dim(values, start, freq_count, 0)

    shell_re, shell_im = (own_rows(ds_re), own_rows(ds_im))
    cavity_re, cavity_im = (own_rows(da_re), own_rows(da_im))
    base_re, base_im = (own_rows(free_re), own_rows(free_im))
    own_squared = own_rows(squared)
    coupled_re = jnp.zeros_like(base_re)
    coupled_im = jnp.zeros_like(base_im)
    for section in range(SECTIONS):
        amounts = jnp.concatenate([base_re + coupled_re, base_im + coupled_im], 0)
        loads = jnp.dot(amounts, coupling.T, precision=HIGH)
        struct_re, struct_im = divide_complex(
            modal_force[None, :] + loads[:freq_count], loads[freq_count:], shell_re, shell_im
        )
        back = jnp.dot(jnp.concatenate([struct_re, struct_im], 0), coupling, precision=HIGH)
        coupled_re, coupled_im = divide_complex(
            own_squared * back[:freq_count], own_squared * back[freq_count:], cavity_re, cavity_im
        )
    mine = jnp.stack([coupled_re, coupled_im]).astype(jnp.bfloat16)
    coupled_amps = lax.all_gather(mine, "grp", axis=1, tiled=True).reshape(2 * freq_total, -1)
    modal_structure = jnp.stack([struct_re, struct_im])
    coupled_field = lax.dot_general(
        acoustic_modes, coupled_amps, (((1,), (1,)), ((), ())), preferred_element_type=jnp.float32
    )
    pressure = (free_field + coupled_field).astype(jnp.bfloat16)
    return (pressure, modal_structure)


def solution(mesh):
    placed = (
        P(("fluid", "grp"), None),
        P("fluid", None),
        P(("fluid", "grp")),
        P(("fluid", "grp")),
        P(("fluid", "grp")),
        P(("fluid", "grp")),
        P(),
        P(),
        P(),
        P(),
        P(),
        P(),
        P(),
    )
    return jax.shard_map(
        on_device,
        mesh=mesh,
        in_specs=placed,
        out_specs=(P(("fluid", "grp"), None), P(None, "grp", None)),
        check_vma=False,
    )
```

profile of v0, /device:TPU:0, one launch (start us, length us, event | category | flops | bytes accessed | tf_op | source)
XLA Modules:
  0.0 214.8 jit_solution(2672962643485708296)
XLA Ops:
  7.2 0.0 all-reduce.2.cloned.1.call-start
  7.9 0.0 copy-start.6
  7.9 10.7 %copy.19 = bf16[8192,400]{1,0:T(8,128)(2,1)} copy(bf16[8192,400]{0,1:T(8,128)(2,1)} %param.15) | data formatting | bytes 13107200 | tf_op args[0]
  18.6 0.0 copy-start.4
  18.6 12.1 %gather_fusion.1 = bf16[2048,400]{1,0:T(8,128)(2,1)S(1)} fusion(bf16[8192,400]{1,0:T(8,128)(2,1)} %copy.19, s32[2048]{0:T(1024)S(1)} %fusion.69), kind=kCustom, calls=%fused_computation.1 | custom fusion | bytes 3284992 | tf_op jit(solution)/shard_map/gather | solution.py:73
  30.7 1.7 fusion.6
  32.4 2.8 %copy.21 = bf16[2048,1,400]{0,2,1:T(8,128)(2,1)S(1)} copy(bf16[2048,1,400]{2,0,1:T(8,128)(2,1)} %fusion.6) | data formatting | bytes 3276800 | tf_op jit(solution)/shard_map/while | solution.py:46
  35.2 1.4 copy.20
  36.7 0.0 copy-start.11
  36.7 0.0 copy-start.7
  36.7 0.0 copy-start.8
  36.7 0.0 copy-start.5
  36.7 4.4 %while.10 = (s32[]{:T(128)}, f32[300,400]{0,1:T(8,128)S(1)}, s32[]{:T(128)}, s32[2048,1]{0,1:T(1,128)}, bf16[1024,300]{1,0:T(8,128)(2,1)S(1)}, /*index=5*/bf16[2...) while((s32[]{:T(128)}, f32[300,400]{0,1:T(8,128)S(1)}, s32[]{:T(128)}, ...), condition=%wide.region_1.2_spmd, body=%wide.region_0.1_spmd.sunk | while | flops 61561796 | bytes 1811355 | solution.py:46
  36.8 0.7 compare_select_fusion.3
  37.5 1.2 gather_fusion
  38.6 0.3 convolution_add_fusion.3
  39.0 0.7 compare_select_fusion.3
  39.7 1.2 gather_fusion
  40.8 0.3 convolution_add_fusion.3
  41.1 0.0 copy-start.1
  41.2 0.8 copy-done.1
  42.0 0.0 all-reduce.2.cloned.1.call-update
  42.1 0.1 fusion.8
  42.2 0.0 copy-start.10
  42.2 0.0 copy-start.3
  42.2 6.2 %fusion.12 = f32[128,8192]{1,0:T(8,128)} fusion(bf16[8192,400]{0,1:T(8,128)(2,1)} %param.15, bf16[64,400]{1,0:T(8,128)(2,1)S(1)} %get-tuple-element.88, bf16[64,400]{1,0:T(8,128)(2,1)S(1)} %get-tuple-element.85), kind=kOutput, calls=%fused_computation.22 | convolution fusion | flops 839065600 | bytes 10850304 | tf_op jit(solution)/shard_map/dot_general | solution.py:82
  48.4 0.1 dynamic-slice.5
  48.5 136.0 %all-reduce.2.cloned.1.call-done = f32[300,400]{0,1:T(8,128)} async-done(((f32[300,400]{0,1:T(8,128)}), f32[300,400]{0,1:T(8,128)}) %all-reduce.2.cloned.1.call-update) | async-done | bytes 480016 | tf_op jit(solution)/shard_map/psum | solution.py:86
  184.5 1.7 fusion.16
  186.2 0.1 fusion.51
  186.3 1.8 fusion.32
  188.0 0.1 divide_add_fusion.5
  188.1 1.5 fusion.20
  189.6 0.1 fusion.57
  189.7 1.8 fusion.36
  191.5 0.1 divide_add_fusion.3
  191.6 1.5 fusion.24
  193.1 0.1 fusion.55
  193.2 0.7 fusion.40
  193.9 0.1 divide_add_fusion.1
  194.0 0.4 fusion.28
  194.4 0.1 fusion.53
  194.5 0.7 fusion.44
  195.2 0.1 fusion.66
  195.3 5.4 %all_gather.3 = bf16[2,64,400]{2,1,0:T(8,128)(2,1)S(1)} all-gather(bf16[2,16,400]{2,1,0:T(8,128)(2,1)S(1)} %pad_maximum_fusion.1), channel_id=1, replica_groups=mesh['fluid'=8,'grp'=4] {'grp'}, dimensions={1}, use_global_device_ids=true | all-gather | bytes 128000 | tf_op jit(solution)/shard_map/all_gather | solution.py:109
  200.7 4.1 %fusion.4 = bf16[8192,128]{0,1:T(8,128)(2,1)S(1)} fusion(f32[128,8192]{1,0:T(8,128)S(1)} %copy-done.2, bf16[128,400]{1,0:T(8,128)(2,1)S(1)} %bitcast.38, bf16[8192,400]{0,1:T(8,128)(2,1)} %param.15), kind=kOutput, calls=%fused_computation.10 | convolution fusion | flops 840957952 | bytes 12947456 | tf_op jit(solution)/shard_map/dot_general | solution.py:111
  204.8 2.4 %copy.22 = bf16[8192,128]{1,0:T(8,128)(2,1)} copy(bf16[8192,128]{0,1:T(8,128)(2,1)S(1)} %fusion.4) | data formatting | bytes 4194304
  207.3 0.6 pad_maximum_fusion
  (25 shorter events, 0.1 us)
Async XLA Ops:
  7.2 177.3 %all-reduce.2.cloned.1.call-start = ((), (), s32[]{:S(2)}) async-start(), calls=%async_computation | async-start | bytes 1228800 | tf_op jit(solution)/shard_map/psum | solution.py:86
  7.9 10.7 %copy-start.6 = (s32[2048]{0:T(1024)S(1)}, s32[2048]{0:T(1024)}, u32[]{:S(2)}) copy-start(s32[2048]{0:T(1024)} %param.18) | copy-start | bytes 24580
  18.6 12.1 %copy-start.4 = (f32[2048]{0:T(1024)S(1)}, f32[2048]{0:T(1024)}, u32[]{:S(2)}) copy-start(f32[2048]{0:T(1024)} %param.20) | copy-start | bytes 24580
  36.7 5.3 %copy-start.11 = (f32[64]{0:T(128)S(1)}, f32[64]{0:T(128)}, u32[]{:S(2)}) copy-start(f32[64]{0:T(128)} %param.25) | copy-start | bytes 772
  36.7 5.3 %copy-start.7 = (f32[400]{0:T(512)S(1)}, f32[400]{0:T(512)}, u32[]{:S(2)}) copy-start(f32[400]{0:T(512)} %param.24) | copy-start | bytes 4804
  36.7 5.3 %copy-start.8 = (f32[400]{0:T(512)S(1)}, f32[400]{0:T(512)}, u32[]{:S(2)}) copy-start(f32[400]{0:T(512)} %param.23) | copy-start | bytes 4804
  36.7 5.3 %copy-start.5 = (f32[400]{0:T(512)S(1)}, f32[400]{0:T(512)}, u32[]{:S(2)}) copy-start(f32[400]{0:T(512)} %param.27) | copy-start | bytes 4804
  41.1 0.8 copy-start.1
  42.2 6.3 %copy-start.9 = (f32[300]{0:T(512)S(1)}, f32[300]{0:T(512)}, u32[]{:S(2)}) copy-start(f32[300]{0:T(512)} %param.22) | copy-start | bytes 3604
  42.2 6.3 %copy-start.10 = (f32[300]{0:T(512)S(1)}, f32[300]{0:T(512)}, u32[]{:S(2)}) copy-start(f32[300]{0:T(512)} %param.21) | copy-start | bytes 3604
  42.2 143.9 %copy-start.3 = (f32[300]{0:T(512)S(1)}, f32[300]{0:T(512)}, u32[]{:S(2)}) copy-start(f32[300]{0:T(512)} %param.26) | copy-start | bytes 3604
  184.5 8.7 %copy-start = (f32[300,400]{0,1:T(8,128)S(1)}, f32[300,400]{0,1:T(8,128)}, u32[]{:S(2)}) copy-start(f32[300,400]{0,1:T(8,128)} %all-reduce.2.cloned.1.call-done) | copy-start | bytes 1440004
  184.5 16.2 %copy-start.2 = (f32[128,8192]{1,0:T(8,128)S(1)}, f32[128,8192]{1,0:T(8,128)}, u32[]{:S(2)}) copy-start(f32[128,8192]{1,0:T(8,128)} %fusion.12) | copy-start | bytes 12582916
Sparse Core Ops, SparseCore 0:
  42.1 142.3 all-reduce.1
where the time goes:
time: 216 us; the launch traced here: 215 us
  waiting for transfers between devices  136 us (63%)
  local copies, waits for them, and re-layouts  32.8 us (15%)
  matrix products  20.8 us (10%)
  between operations  15 us (7%)
  blocking collectives  5.42 us (3%)
  other arithmetic  4.57 us (2%)
    psum x1, waiting for transfers between devices, on_device(): coupling = lax.psum(partial_sum, ('fluid', 'grp'))  136 us
    unnamed x26, local copies, waits for them, and re-layouts  14 us
    gather x1, local copies, waits for them, and re-layouts, on_device(): acoustic_modes[fluid_nodes].astype(jnp.float32)  12.1 us
    dot_general x1, matrix products, on_device(): lax.dot_general(acoustic_modes, free_amps, (((1,), (1,)), ((), ())), pref...  6.15 us
    all_gather x1, blocking collectives, on_device(): lax.all_gather(mine, 'grp', axis=1, tiled=True).reshape(2 * freq_total, -1)  5.42 us
    dot_general x4, matrix products, on_device(): loads = jnp.dot(amounts, coupling.T, precision=HIGH)  5.1 us
    dot_general x4, matrix products, on_device(): jnp.dot(jnp.concatenate([struct_re, struct_im], 0), coupling, precision=H...  4.87 us
  transfers between devices with their start and end apart: 1, of which 1 were waited for; matrix products, arithmetic and copies ran while one was open for 3% of the time, Pallas kernels for 0%

commit v1 on v0

v1 whole, which is shorter than its diff:
```python
import functools

import jax
import jax.numpy as jnp
from jax import lax
from jax.experimental import pallas as pl
from jax.experimental.pallas import tpu as pltpu
from jax.sharding import PartitionSpec as P

SECTIONS = 4
LANES = 128
SLOT_BLOCK = 256
F32 = jnp.float32
BF16 = jnp.bfloat16


def ceil_to(value, step):
    return (value + step - 1) // step * step


def divide_complex(real_part, imag_part, denom_real, denom_imag):
    scale = 1.0 / (denom_real * denom_real + denom_imag * denom_imag)
    return (
        (real_part * denom_real + imag_part * denom_imag) * scale,
        (imag_part * denom_real - real_part * denom_imag) * scale,
    )


class Packing:
    def __init__(self, rows, columns, parts):
        self.rows, self.columns = rows, columns
        self.padded = ceil_to(rows, 8)
        self.full, self.tail = columns // LANES, columns % LANES
        self.pieces = LANES // self.tail if self.tail else 1
        self.group = ceil_to(-(-self.padded // self.pieces), 8) if self.tail else 0
        self.total = ceil_to(self.padded * self.full + self.group, 16 * parts)

    def store(self, out_ref, matrix):
        for j in range(self.full):
            out_ref[pl.ds(j * self.padded, self.padded), :] = matrix[
                :, j * LANES : (j + 1) * LANES
            ].astype(out_ref.dtype)
        first = self.full * self.padded
        if self.tail:
            rest = matrix[:, self.full * LANES :]
            packed = None
            for piece in range(self.pieces):
                low = piece * self.group
                high = min(low + self.group, self.padded)
                if low >= high:
                    break
                part = rest[low:high]
                if high - low < self.group:
                    part = jnp.concatenate(
                        [part, jnp.zeros((self.group - (high - low), LANES), part.dtype)], 0
                    )
                if piece:
                    part = pltpu.roll(part, piece * self.tail, 1)
                packed = part if packed is None else packed + part
            out_ref[pl.ds(first, self.group), :] = packed.astype(out_ref.dtype)
            first += self.group
        if first < self.total:
            out_ref[pl.ds(first, self.total - first), :] = jnp.zeros(
                (self.total - first, LANES), out_ref.dtype
            )

    def load(self, values):
        tiles = [values[j * self.padded : (j + 1) * self.padded] for j in range(self.full)]
        if self.tail:
            first = self.full * self.padded
            packed = values[first : first + self.group]
            lane = lax.broadcasted_iota(jnp.int32, packed.shape, 1)
            parts = []
            for piece in range(self.pieces):
                low = piece * self.group
                high = min(low + self.group, self.padded)
                if low >= high:
                    break
                part = pltpu.roll(packed, (LANES - piece * self.tail) % LANES, 1) if piece else packed
                part = jnp.where(lane < self.tail, part, 0.0)
                parts.append(part[: high - low])
            tiles.append(jnp.concatenate(parts, 0))
        return jnp.concatenate(tiles, 1)


def couple_kernel(
    packing,
    count_ref,
    nodes_ref,
    modes_ref,
    shell_ref,
    shell_nodes_ref,
    area_ref,
    out_ref,
    flat_ref,
    table,
    picked,
):
    step = pl.program_id(0)
    cavity, width = modes_ref.shape
    pad = table.shape[1] * LANES
    piece = 256

    row = lax.broadcasted_iota(jnp.int32, (piece, piece), 0)
    col = lax.broadcasted_iota(jnp.int32, (piece, piece), 1)
    unit = (row == col).astype(BF16)
    for part in range(width // piece):
        block = modes_ref[:, part * piece : (part + 1) * piece]
        turned = lax.dot_general(
            unit, block, (((1,), (1,)), ((), ())), preferred_element_type=F32
        )
        flat_ref[pl.ds(part * piece, piece), :] = turned.astype(BF16)
        turned = jnp.concatenate([turned, jnp.zeros((piece, pad - cavity), F32)], 1)
        at = pl.multiple_of(step * width + part * piece, piece)
        for j in range(table.shape[1]):
            table[pl.ds(at, piece), j, :] = turned[:, j * LANES : (j + 1) * LANES]

    @pl.when(step == pl.num_programs(0) - 1)
    def _():
        count = count_ref[0]
        shell = shell_ref[...]
        nodes, modes = shell.shape[1], shell.shape[0]

        def add_block(number, total):
            base = pl.multiple_of(number * SLOT_BLOCK, SLOT_BLOCK)

            def pick(group, _):
                first = group * 16
                for slot in range(16):
                    picked[first + slot] = table[nodes_ref[base + first + slot]]
                return 0

            lax.fori_loop(0, SLOT_BLOCK // 16, pick, 0)
            rows = jnp.concatenate(
                [picked[:, j, :] for j in range(table.shape[1])], 1
            ).astype(BF16)
            ids = shell_nodes_ref[:, pl.ds(base, SLOT_BLOCK)]
            chosen = lax.broadcasted_iota(jnp.int32, (nodes, SLOT_BLOCK), 0) == ids
            shell_rows = jnp.dot(shell, chosen.astype(BF16), preferred_element_type=F32)
            slot = base + lax.broadcasted_iota(jnp.int32, (1, SLOT_BLOCK), 1)
            weight = jnp.where(slot < count, area_ref[:, pl.ds(base, SLOT_BLOCK)], 0.0)
            scaled = (shell_rows * weight).astype(BF16)
            return total + jnp.dot(scaled, rows, preferred_element_type=F32)

        total = lax.fori_loop(
            0,
            (count + SLOT_BLOCK - 1) // SLOT_BLOCK,
            add_block,
            jnp.zeros((modes, pad), F32),
        )
        total = jnp.concatenate(
            [total, jnp.zeros((packing.padded - modes, pad), F32)], 0
        )
        packing.store(out_ref, total)


def couple(packing, count, nodes, modes_t, shell_t, shell_nodes, area, width):
    cavity, dofs = modes_t.shape
    tiles = -(-cavity // LANES)
    smem = pl.BlockSpec(memory_space=pltpu.SMEM)
    whole = lambda a: pl.BlockSpec(a.shape, lambda i: (0, 0))
    return pl.pallas_call(
        functools.partial(couple_kernel, packing),
        grid=(dofs // width,),
        in_specs=[
            smem,
            smem,
            pl.BlockSpec((cavity, width), lambda i: (0, i)),
            whole(shell_t),
            whole(shell_nodes),
            whole(area),
        ],
        out_specs=[
            pl.BlockSpec((packing.total, LANES), lambda i: (0, 0)),
            pl.BlockSpec((width, cavity), lambda i: (i, 0)),
        ],
        out_shape=[
            jax.ShapeDtypeStruct((packing.total, LANES), BF16),
            jax.ShapeDtypeStruct((dofs, cavity), BF16),
        ],
        scratch_shapes=[
            pltpu.VMEM((dofs, tiles, LANES), F32),
            pltpu.VMEM((SLOT_BLOCK, tiles, LANES), F32),
        ],
        name="couple",
    )(count, nodes, modes_t, shell_t, shell_nodes, area)


def split_dot(values, matrix, dims):
    rows = values.shape[0]
    high = values.astype(BF16)
    low = (values - high.astype(F32)).astype(BF16)
    both = lax.dot_general(
        jnp.concatenate([high, low], 0), matrix, (dims, ((), ())), preferred_element_type=F32
    )
    return both[:rows] + both[rows:]


def recover_kernel(
    packing,
    member_ref,
    coupling_ref,
    shell_freq_ref,
    shell_loss_ref,
    cavity_freq_ref,
    cavity_loss_ref,
    freqs_ref,
    force_ref,
    source_ref,
    flat_ref,
    pressure_ref,
    struct_ref,
    weights,
    structure,
):
    count = freqs_ref.shape[1]
    own = struct_ref.shape[1]

    @pl.when(pl.program_id(0) == 0)
    def _():
        matrix = packing.load(coupling_ref[...].astype(F32))
        matrix = matrix[: packing.rows, : packing.columns].astype(BF16)
        row = lax.broadcasted_iota(jnp.int32, (count, count), 0)
        col = lax.broadcasted_iota(jnp.int32, (count, count), 1)
        freqs = jnp.sum(jnp.where(row == col, freqs_ref[...], 0.0), 1, keepdims=True)
        squared = freqs * freqs

        def terms(freq_ref, loss_ref):
            stiff = freq_ref[...] * freq_ref[...]
            real_part = stiff - squared
            imag_part = jnp.broadcast_to(loss_ref[...] * stiff, real_part.shape)
            scale = 1.0 / (real_part * real_part + imag_part * imag_part)
            return real_part * scale, imag_part * scale

        ds_re, ds_im = terms(shell_freq_ref, shell_loss_ref)
        da_re, da_im = terms(cavity_freq_ref, cavity_loss_ref)
        free_re = source_ref[...] * da_re
        free_im = -source_ref[...] * da_im
        wa_re, wa_im = squared * da_re, squared * da_im
        free = jnp.concatenate([free_re, free_im], 0)
        amounts = free
        force = force_ref[...]
        for section in range(SECTIONS):
            loads = split_dot(amounts, matrix, ((1,), (1,)))
            load_re, load_im = force + loads[:count], loads[count:]
            struct_re = load_re * ds_re + load_im * ds_im
            struct_im = load_im * ds_re - load_re * ds_im
            back = split_dot(jnp.concatenate([struct_re, struct_im], 0), matrix, ((1,), (0,)))
            back_re, back_im = back[:count], back[count:]
            coupled = jnp.concatenate(
                [back_re * wa_re + back_im * wa_im, back_im * wa_re - back_re * wa_im], 0
            )
            amounts = free + coupled
        weights[...] = jnp.concatenate([free.astype(BF16), coupled.astype(BF16)], 0)
        structure[0] = struct_re
        structure[1] = struct_im
        start = pl.multiple_of(member_ref[0] * own, own)
        struct_ref[...] = structure[:, pl.ds(start, own), :]

    both = lax.dot_general(
        flat_ref[...], weights[...], (((1,), (1,)), ((), ())), preferred_element_type=F32
    )
    pressure_ref[...] = (both[:, : 2 * count] + both[:, 2 * count :]).astype(BF16)


def recover(packing, groups, member, coupling, vectors, flat, width):
    dofs, cavity = flat.shape
    shell_freq, shell_loss, cavity_freq, cavity_loss, freqs, force, source = vectors
    count = freqs.shape[1]
    whole = lambda a: pl.BlockSpec(a.shape, lambda i: (0, 0))
    return pl.pallas_call(
        functools.partial(recover_kernel, packing),
        grid=(dofs // width,),
        in_specs=[pl.BlockSpec(memory_space=pltpu.SMEM), whole(coupling)]
        + [whole(v) for v in vectors]
        + [pl.BlockSpec((width, cavity), lambda i: (i, 0))],
        out_specs=[
            pl.BlockSpec((width, 2 * count), lambda i: (i, 0)),
            pl.BlockSpec((2, count // groups, packing.rows), lambda i: (0, 0, 0)),
        ],
        out_shape=[
            jax.ShapeDtypeStruct((dofs, 2 * count), BF16),
            jax.ShapeDtypeStruct((2, count // groups, packing.rows), F32),
        ],
        scratch_shapes=[
            pltpu.VMEM((4 * count, cavity), BF16),
            pltpu.VMEM((2, count, packing.rows), F32),
        ],
        name="recover",
    )(member, coupling, *vectors, flat)


def partner(axis, bit):
    return [(i, i ^ bit) for i in range(lax.axis_size(axis))]


def halve(values, axis, bit):
    half = values.shape[0] // 2
    upper = (lax.axis_index(axis) & bit) != 0
    sent = jnp.where(upper, values[:half], values[half:])
    kept = jnp.where(upper, values[half:], values[:half])
    got = lax.ppermute(sent.astype(BF16), axis, partner(axis, bit))
    return kept.astype(F32) + got.astype(F32)


def exchange(values, axis, bit):
    mine = values.astype(BF16)
    return mine.astype(F32) + lax.ppermute(mine, axis, partner(axis, bit)).astype(F32)


def rejoin(values, axis, bit):
    mine = values.astype(BF16)
    upper = (lax.axis_index(axis) & bit) != 0
    got = lax.ppermute(mine, axis, partner(axis, bit))
    return jnp.concatenate([jnp.where(upper, got, mine), jnp.where(upper, mine, got)], 0)


def bits_of(size):
    return [1 << k for k in range(size.bit_length() - 1)]


def sum_everywhere(values):
    group_bits = bits_of(lax.axis_size("grp"))
    for bit in group_bits:
        values = halve(values, "grp", bit)
    for bit in bits_of(lax.axis_size("fluid")):
        values = exchange(values, "fluid", bit)
    for bit in reversed(group_bits):
        values = rejoin(values, "grp", bit)
    return values


def on_device(
    acoustic_modes,
    shell_modes,
    wet_counts,
    fluid_nodes,
    shell_nodes,
    wet_area,
    shell_freq,
    shell_loss,
    cavity_freq,
    cavity_loss,
    freqs,
    modal_force,
    cavity_source,
):
    groups = lax.axis_size("grp")
    member = lax.axis_index("grp").astype(jnp.int32).reshape(1)
    packing = Packing(shell_modes.shape[1], acoustic_modes.shape[1], groups)
    partial_sum, flat = couple(
        packing,
        wet_counts,
        fluid_nodes,
        acoustic_modes.T,
        shell_modes.T,
        shell_nodes[None, :],
        wet_area[None, :],
        512,
    )
    coupling = sum_everywhere(partial_sum)
    vectors = [
        v[None, :]
        for v in (
            shell_freq,
            shell_loss,
            cavity_freq,
            cavity_loss,
            freqs,
            modal_force,
            cavity_source,
        )
    ]
    return tuple(recover(packing, groups, member, coupling, vectors, flat, 1024))


def solution(mesh):
    assert mesh.shape["fluid"] & (mesh.shape["fluid"] - 1) == 0
    assert mesh.shape["grp"] & (mesh.shape["grp"] - 1) == 0
    placed = (
        P(("fluid", "grp"), None),
        P("fluid", None),
        P(("fluid", "grp")),
        P(("fluid", "grp")),
        P(("fluid", "grp")),
        P(("fluid", "grp")),
        P(),
        P(),
        P(),
        P(),
        P(),
        P(),
        P(),
    )
    return jax.shard_map(
        on_device,
        mesh=mesh,
        in_specs=placed,
        out_specs=(P(("fluid", "grp"), None), P(None, "grp", None)),
        check_vma=False,
    )
```

time: 216 us -> 69.4 us (0.32)
  waiting for transfers between devices: 136 us -> 14.2 us
  Pallas kernels: 0 us -> 31.3 us
  local copies, waits for them, and re-layouts: 32.8 us -> 1.77 us
  matrix products: 20.8 us -> 0 us
  starting transfers between devices: 0.04 us -> 16.5 us
  between operations: 15 us -> 1.41 us
  blocking collectives: 5.42 us -> 0 us
    psum x1 -> x0, waiting for transfers between devices: 136 us -> none  [on_device(): coupling = lax.psum(partial_sum, ('fluid', 'grp'))]
    pallas_call x0 -> x2, Pallas kernels: none -> 31.3 us  [the longest x1 20.3 us: couple(): pl.pallas_call(functools.partial(couple_kernel, packing), grid=(dofs // w...]
    dot_general x12 -> x0, matrix products: 20.8 us -> none  [the longest x1 6.15 us: on_device(): lax.dot_general(acoustic_modes, free_amps, (((1,), (1,)), ((), ())), pref...]
    ppermute x0 -> x7, starting transfers between devices: none -> 16.5 us  [the longest x3 9.09 us: exchange(): lax.ppermute(mine, axis, partner(axis, bit)).astype(F32)]
    gather x3 -> x0, local copies, waits for them, and re-layouts: 14.4 us -> none  [the longest x1 12.1 us: on_device(): acoustic_modes[fluid_nodes].astype(jnp.float32)]
    ppermute x0 -> x7, waiting for transfers between devices: none -> 14.2 us  [the longest x3 7.62 us: exchange(): lax.ppermute(mine, axis, partner(axis, bit)).astype(F32)]
    unnamed x26 -> x6, local copies, waits for them, and re-layouts: 14 us -> 0.01 us
    all_gather x1 -> x0, blocking collectives: 5.42 us -> none  [on_device(): lax.all_gather(mine, 'grp', axis=1, tiled=True).reshape(2 * freq_total, -1)]
  transfers between devices with their start and end apart: 1 -> 7, of which waited for: 1 -> 6; matrix products, arithmetic and copies ran while one was open for 3% -> 3% of each run, Pallas kernels for 0% -> 0%
where the time goes in v1:
time: 69.4 us; the launch traced here: 68.1 us
  Pallas kernels  31.3 us (45%)
  starting transfers between devices  16.5 us (24%)
  waiting for transfers between devices  14.2 us (20%)
  other arithmetic  2.88 us (4%)
  local copies, waits for them, and re-layouts  1.77 us (3%)
  between operations  1.41 us (2%)
    pallas_call x1, Pallas kernels, couple(): pl.pallas_call(functools.partial(couple_kernel, packing), grid=(dofs // w...  20.3 us
    pallas_call x1, Pallas kernels, recover(): pl.pallas_call(functools.partial(recover_kernel, packing), grid=(dofs //...  11 us
    ppermute x3, starting transfers between devices, exchange(): lax.ppermute(mine, axis, partner(axis, bit)).astype(F32)  9.09 us
    ppermute x3, waiting for transfers between devices, exchange(): lax.ppermute(mine, axis, partner(axis, bit)).astype(F32)  7.62 us
    ppermute x2, starting transfers between devices, halve(): got = lax.ppermute(sent.astype(BF16), axis, partner(axis, bit))  5.79 us
    ppermute x2, waiting for transfers between devices, halve(): got = lax.ppermute(sent.astype(BF16), axis, partner(axis, bit))  3.85 us
    ppermute x2, waiting for transfers between devices, rejoin(): got = lax.ppermute(mine, axis, partner(axis, bit))  2.73 us
    broadcast_in_dim x3, local copies, waits for them, and re-layouts, on_device(): v[None, :]  1.75 us
  transfers between devices with their start and end apart: 7, of which 6 were waited for; matrix products, arithmetic and copies ran while one was open for 3% of the time, Pallas kernels for 0%

profile of v1, /device:TPU:0, one launch (start us, length us, event | category | flops | bytes accessed | tf_op | source)
XLA Modules:
  0.0 68.1 jit_solution(15150233545815795974)
XLA Ops:
  0.6 0.0 copy-start
  0.6 0.0 copy-start.1
  0.7 0.0 copy-start.2
  1.3 20.3 %couple.1 = (bf16[960,128]{1,0:T(8,128)(2,1)}, bf16[8192,400]{1,0:T(8,128)(2,1)}) custom-call(s32[1]{0:T(128)S(6)} %copy.15.count_ref, s32[2048]{0:T(1024)} %nodes_ref.1, bf16[400,8192]{1,0:T(8,128)(2,1)} %bitcast.9, bf16[300,1024]{1,0:T(8,128)(2,1)} %bitcast.10, s32[1,2048]{1,0:T(1,128)} %bitcast.11, f32[1,2048]{1,0:T(1,128)} %bitcast.12), custom_call_target="tpu_custom_call" | custom-call | tf_op jit(solution)/shard_map/couple/pallas_call | solution.py:162
  21.6 1.0 %broadcast_select_fusion.2 = bf16[480,128]{1,0:T(8,128)(2,1)S(1)} fusion(pred[]{:T(512)S(6)} %ne.8, bf16[960,128]{1,0:T(8,128)(2,1)} %get-tuple-element.4), kind=kLoop, calls=%fused_computation.10 | loop fusion | flops 61440 | bytes 368641 | tf_op jit(solution)/shard_map/jit(_where)/select_n | solution.py:300
  22.6 0.1 collective-permute-start
  22.7 1.3 %collective-permute-done = bf16[480,128]{1,0:T(8,128)(2,1)S(1)} collective-permute-done((bf16[480,128]{1,0:T(8,128)(2,1)S(1)}, bf16[480,128]{1,0:T(8,128)(2,1)S(1)}, u32[]{:S(2)}, u32[]{:S(2)}) %collective-permute-start) | collective-permute-done | bytes 122912 | tf_op jit(solution)/shard_map/ppermute | solution.py:302
  24.0 1.0 %convert_add_fusion = f32[480,128]{1,0:T(8,128)S(1)} fusion(bf16[480,128]{1,0:T(8,128)(2,1)S(1)} %collective-permute-done, pred[]{:T(512)S(6)} %ne.8, bf16[960,128]{1,0:T(8,128)(2,1)} %get-tuple-element.4), kind=kLoop, calls=%fused_computation.1 | loop fusion | flops 245760 | bytes 614401 | tf_op jit(solution)/shard_map/add | solution.py:303
  25.0 5.7 %collective-permute-start.1 = (bf16[240,128]{1,0:T(8,128)(2,1)S(1)}, bf16[240,128]{1,0:T(8,128)(2,1)S(1)}, u32[]{:S(2)}, u32[]{:S(2)}) collective-permute-start(bf16[240,128]{1,0:T(8,128)(2,1)S(1)} %select_convert_fusion), channel_id=1, source_target_pairs={{0,2},{1,3},{2,0},{3,1},{4,6},{5,7},{6,4},{7,5},{8,10},{9,11},{10,... | collective-permute-start | bytes 184328 | tf_op jit(solution)/shard_map/ppermute | solution.py:302
  30.8 2.5 %collective-permute-done.1 = bf16[240,128]{1,0:T(8,128)(2,1)S(1)} collective-permute-done((bf16[240,128]{1,0:T(8,128)(2,1)S(1)}, bf16[240,128]{1,0:T(8,128)(2,1)S(1)}, u32[]{:S(2)}, u32[]{:S(2)}) %collective-permute-start.1) | collective-permute-done | bytes 61472 | tf_op jit(solution)/shard_map/ppermute | solution.py:302
  33.3 5.0 %collective-permute-start.2 = (bf16[240,128]{1,0:T(8,128)(2,1)S(1)}, bf16[240,128]{1,0:T(8,128)(2,1)S(1)}, u32[]{:S(2)}, u32[]{:S(2)}) collective-permute-start(bf16[240,128]{1,0:T(8,128)(2,1)S(1)} %add_convert_fusion.3), channel_id=1, source_target_pairs={{0,4},{4,0},{8,12},{12,8},{16,20},{20,16},{24,28},{28,24},{1,5},{5... | collective-permute-start | bytes 184328 | tf_op jit(solution)/shard_map/ppermute | solution.py:308
  38.4 2.2 %collective-permute-done.2 = bf16[240,128]{1,0:T(8,128)(2,1)S(1)} collective-permute-done((bf16[240,128]{1,0:T(8,128)(2,1)S(1)}, bf16[240,128]{1,0:T(8,128)(2,1)S(1)}, u32[]{:S(2)}, u32[]{:S(2)}) %collective-permute-start.2) | collective-permute-done | bytes 61472 | tf_op jit(solution)/shard_map/ppermute | solution.py:308
  40.6 1.4 %collective-permute-start.3 = (bf16[240,128]{1,0:T(8,128)(2,1)S(1)}, bf16[240,128]{1,0:T(8,128)(2,1)S(1)}, u32[]{:S(2)}, u32[]{:S(2)}) collective-permute-start(bf16[240,128]{1,0:T(8,128)(2,1)S(1)} %add_convert_fusion.2), channel_id=1, source_target_pairs={{0,8},{4,12},{8,0},{12,4},{16,24},{20,28},{24,16},{28,20},{1,9},{5... | collective-permute-start | bytes 184328 | tf_op jit(solution)/shard_map/ppermute | solution.py:308
  42.0 2.9 %collective-permute-done.3 = bf16[240,128]{1,0:T(8,128)(2,1)S(1)} collective-permute-done((bf16[240,128]{1,0:T(8,128)(2,1)S(1)}, bf16[240,128]{1,0:T(8,128)(2,1)S(1)}, u32[]{:S(2)}, u32[]{:S(2)}) %collective-permute-start.3) | collective-permute-done | bytes 61472 | tf_op jit(solution)/shard_map/ppermute | solution.py:308
  44.9 2.7 %collective-permute-start.4 = (bf16[240,128]{1,0:T(8,128)(2,1)S(1)}, bf16[240,128]{1,0:T(8,128)(2,1)S(1)}, u32[]{:S(2)}, u32[]{:S(2)}) collective-permute-start(bf16[240,128]{1,0:T(8,128)(2,1)S(1)} %add_convert_fusion.1), channel_id=1, source_target_pairs={{0,16},{4,20},{8,24},{12,28},{16,0},{20,4},{24,8},{28,12},{1,17},{... | collective-permute-start | bytes 184328 | tf_op jit(solution)/shard_map/ppermute | solution.py:308
  47.5 2.5 %collective-permute-done.4 = bf16[240,128]{1,0:T(8,128)(2,1)S(1)} collective-permute-done((bf16[240,128]{1,0:T(8,128)(2,1)S(1)}, bf16[240,128]{1,0:T(8,128)(2,1)S(1)}, u32[]{:S(2)}, u32[]{:S(2)}) %collective-permute-start.4) | collective-permute-done | bytes 61472 | tf_op jit(solution)/shard_map/ppermute | solution.py:308
  50.1 1.6 %collective-permute-start.5 = (bf16[240,128]{1,0:T(8,128)(2,1)S(1)}, bf16[240,128]{1,0:T(8,128)(2,1)S(1)}, u32[]{:S(2)}, u32[]{:S(2)}) collective-permute-start(bf16[240,128]{1,0:T(8,128)(2,1)S(1)} %add_convert_fusion), channel_id=1, source_target_pairs={{0,2},{1,3},{2,0},{3,1},{4,6},{5,7},{6,4},{7,5},{8,10},{9,11},{10,... | collective-permute-start | bytes 184328 | tf_op jit(solution)/shard_map/ppermute | solution.py:314
  51.7 2.7 %collective-permute-done.5 = bf16[240,128]{1,0:T(8,128)(2,1)S(1)} collective-permute-done((bf16[240,128]{1,0:T(8,128)(2,1)S(1)}, bf16[240,128]{1,0:T(8,128)(2,1)S(1)}, u32[]{:S(2)}, u32[]{:S(2)}) %collective-permute-start.5) | collective-permute-done | bytes 61472 | tf_op jit(solution)/shard_map/ppermute | solution.py:314
  54.4 0.1 collective-permute-start.6
  54.5 0.0 copy-done
  54.5 0.6 broadcast_in_dim.29.shell_freq_ref
  55.1 0.0 copy-done.1
  55.1 0.6 broadcast_in_dim.30.shell_loss_ref
  55.7 0.0 copy-done.2
  55.7 0.6 broadcast_in_dim.34.force_ref
  56.3 0.0 collective-permute-done.6
  56.3 0.1 broadcast_select_fusion.1
  56.3 0.7 %pad_maximum_fusion.coupling_ref = bf16[960,128]{1,0:T(8,128)(2,1)} fusion(bf16[480,128]{1,0:T(8,128)(2,1)S(1)} %get-tuple-element.7, bf16[480,128]{1,0:T(8,128)(2,1)S(1)} %get-tuple-element.6), kind=kLoop, calls=%fused_computation | loop fusion | flops 491520 | bytes 491520 | tf_op jit(solution)/shard_map/concatenate | solution.py:315
  57.1 11.0 %recover.1 = (bf16[8192,128]{1,0:T(8,128)(2,1)}, f32[2,16,300]{2,1,0:T(8,128)}) custom-call(s32[1]{0:T(128)} %bitcast.member_ref, bf16[960,128]{1,0:T(8,128)(2,1)} %pad_maximum_fusion.coupling_ref, f32[1,300]{1,0:T(1,128)} %broadcast_in_dim.29.shell_freq_ref, f32[1,300]{1,0:T(1,128)} %broadcast_in_dim.30.shell_loss_ref, f32[1,400]{1,0:T(1,128)} %bitcast.13, ...), custom_call_target="tpu_custom_call" | custom-call | tf_op jit(solution)/shard_map/recover/pallas_call | solution.py:271
  (7 shorter events, 0.1 us)
Async XLA Ops:
  0.6 53.9 %copy-start = (f32[300]{0:T(512)S(1)}, f32[300]{0:T(512)}, u32[]{:S(2)}) copy-start(f32[300]{0:T(512)} %param.19) | copy-start | bytes 3604
  0.6 54.4 %copy-start.1 = (f32[300]{0:T(512)S(1)}, f32[300]{0:T(512)}, u32[]{:S(2)}) copy-start(f32[300]{0:T(512)} %param.20) | copy-start | bytes 3604
  0.7 55.0 %copy-start.2 = (f32[300]{0:T(512)S(1)}, f32[300]{0:T(512)}, u32[]{:S(2)}) copy-start(f32[300]{0:T(512)} %param.24) | copy-start | bytes 3604
  22.6 1.4 %collective-permute-start = (bf16[480,128]{1,0:T(8,128)(2,1)S(1)}, bf16[480,128]{1,0:T(8,128)(2,1)S(1)}, u32[]{:S(2)}, u32[]{:S(2)}) collective-permute-start(bf16[480,128]{1,0:T(8,128)(2,1)S(1)} %broadcast_select_fusion.2), channel_id=1, source_target_pairs={{0,1},{1,0},{2,3},{3,2},{4,5},{5,4},{6,7},{7,6},{8,9},{9,8},{10,11... | collective-permute-start | bytes 368648 | tf_op jit(solution)/shard_map/ppermute | solution.py:302
  25.0 8.3 %collective-permute-start.1 = (bf16[240,128]{1,0:T(8,128)(2,1)S(1)}, bf16[240,128]{1,0:T(8,128)(2,1)S(1)}, u32[]{:S(2)}, u32[]{:S(2)}) collective-permute-start(bf16[240,128]{1,0:T(8,128)(2,1)S(1)} %select_convert_fusion), channel_id=1, source_target_pairs={{0,2},{1,3},{2,0},{3,1},{4,6},{5,7},{6,4},{7,5},{8,10},{9,11},{10,... | collective-permute-start | bytes 184328 | tf_op jit(solution)/shard_map/ppermute | solution.py:302
  33.3 7.2 %collective-permute-start.2 = (bf16[240,128]{1,0:T(8,128)(2,1)S(1)}, bf16[240,128]{1,0:T(8,128)(2,1)S(1)}, u32[]{:S(2)}, u32[]{:S(2)}) collective-permute-start(bf16[240,128]{1,0:T(8,128)(2,1)S(1)} %add_convert_fusion.3), channel_id=1, source_target_pairs={{0,4},{4,0},{8,12},{12,8},{16,20},{20,16},{24,28},{28,24},{1,5},{5... | collective-permute-start | bytes 184328 | tf_op jit(solution)/shard_map/ppermute | solution.py:308
  40.6 4.3 %collective-permute-start.3 = (bf16[240,128]{1,0:T(8,128)(2,1)S(1)}, bf16[240,128]{1,0:T(8,128)(2,1)S(1)}, u32[]{:S(2)}, u32[]{:S(2)}) collective-permute-start(bf16[240,128]{1,0:T(8,128)(2,1)S(1)} %add_convert_fusion.2), channel_id=1, source_target_pairs={{0,8},{4,12},{8,0},{12,4},{16,24},{20,28},{24,16},{28,20},{1,9},{5... | collective-permute-start | bytes 184328 | tf_op jit(solution)/shard_map/ppermute | solution.py:308
  44.9 5.2 %collective-permute-start.4 = (bf16[240,128]{1,0:T(8,128)(2,1)S(1)}, bf16[240,128]{1,0:T(8,128)(2,1)S(1)}, u32[]{:S(2)}, u32[]{:S(2)}) collective-permute-start(bf16[240,128]{1,0:T(8,128)(2,1)S(1)} %add_convert_fusion.1), channel_id=1, source_target_pairs={{0,16},{4,20},{8,24},{12,28},{16,0},{20,4},{24,8},{28,12},{1,17},{... | collective-permute-start | bytes 184328 | tf_op jit(solution)/shard_map/ppermute | solution.py:308
  50.1 4.3 %collective-permute-start.5 = (bf16[240,128]{1,0:T(8,128)(2,1)S(1)}, bf16[240,128]{1,0:T(8,128)(2,1)S(1)}, u32[]{:S(2)}, u32[]{:S(2)}) collective-permute-start(bf16[240,128]{1,0:T(8,128)(2,1)S(1)} %add_convert_fusion), channel_id=1, source_target_pairs={{0,2},{1,3},{2,0},{3,1},{4,6},{5,7},{6,4},{7,5},{8,10},{9,11},{10,... | collective-permute-start | bytes 184328 | tf_op jit(solution)/shard_map/ppermute | solution.py:314
  54.4 1.9 %collective-permute-start.6 = (bf16[480,128]{1,0:T(8,128)(2,1)S(1)}, bf16[480,128]{1,0:T(8,128)(2,1)S(1)}, u32[]{:S(2)}, u32[]{:S(2)}) collective-permute-start(bf16[480,128]{1,0:T(8,128)(2,1)S(1)} %pad_maximum_fusion.1), channel_id=1, source_target_pairs={{0,1},{1,0},{2,3},{3,2},{4,5},{5,4},{6,7},{7,6},{8,9},{9,8},{10,11... | collective-permute-start | bytes 368648 | tf_op jit(solution)/shard_map/ppermute | solution.py:314
